TPU v7x, 32 devices: a whole 2x2x4 slice. The times are simulated.
32 devices in a mesh: gx: 4 (over z), gy: 4 (over y, core), gz: 2 (over x).
Axes of the slice: x: 2, y: 2, z: 4, core: 2. Of those that a mesh axis runs over, the one named last changes fastest.
Arguments:
- gradients: bfloat16 [32, 768, 512], P(('gx', 'gy', 'gz')), may hold values from -6 to 6
- master_weights: float32 [768, 512], P(('gx', 'gy', 'gz')), may hold values from -10 to 10
- first_moment: float32 [768, 512], P(('gx', 'gy', 'gz')), may hold values from -8 to 8
- second_moment: float32 [768, 512], P(('gx', 'gy', 'gz')), may hold values from 1 to 100
- tensor_ids: int32 [768], P(('gx', 'gy', 'gz')), may hold values from 0 to 3, as said below
Outputs:
- new_master: float32 [768, 512], P(('gx', 'gy', 'gz'))
- new_first: float32 [768, 512], P(('gx', 'gy', 'gz'))
- new_second: float32 [768, 512], P(('gx', 'gy', 'gz'))
- scaled_update: float32 [768, 512], P(('gx', 'gy', 'gz'))
- params: bfloat16 [768, 512], replicated
Inputs may be any that keep to these rules, and one draw needn't show every extreme that they name: `tensor_ids`: nondecreasing along the rows; every tensor of 4 owns one contiguous run of rows.
All inputs are finite; a program needn't handle non-finite values.
Results may differ from a plain program's by a relative error of at most 0.0045.
Values may be sent and summed in bfloat16 or wider, within the bound.
A program may use at most 64 MiB of HBM per device.

v0:
```python
import jax
import jax.numpy as jnp
from jax import lax
from jax.sharding import PartitionSpec as P

NT = 4
decay_first = 0.9
decay_second = 0.999
epsilon = 1e-06
weight_decay = 0.01
step_size = 0.05


def tensor_sums(values, onehot):
    return jnp.dot(jnp.sum(values * values, axis=1), onehot, precision=lax.Precision.HIGHEST)


def on_device(gradients, master_weights, first_moment, second_moment, tensor_ids):
    count_across = lax.axis_size("gx")
    count_down = lax.axis_size("gy")
    count_along = lax.axis_size("gz")
    own_rows, row_width = master_weights.shape
    own_gradient = gradients[0].astype(jnp.float32)
    onehot = (tensor_ids[:, None] == jnp.arange(NT, dtype=jnp.int32)[None, :]).astype(jnp.float32)
    counts = jnp.sum(onehot, axis=0) * row_width
    weight_local = tensor_sums(master_weights, onehot)
    summed = lax.psum_scatter(own_gradient, ("gx", "gy", "gz"), scatter_dimension=0, tiled=True)
    new_first = decay_first * first_moment + (1.0 - decay_first) * summed
    new_second = decay_second * second_moment + (1.0 - decay_second) * summed * summed
    update = new_first / (jnp.sqrt(new_second) + epsilon) + weight_decay * master_weights
    update_local = tensor_sums(update, onehot)
    weight_sq, update_sq, total_counts = lax.psum(
        (weight_local, update_local, counts), ("gx", "gy", "gz")
    )
    trust_ratio = jnp.sqrt(weight_sq / (update_sq + total_counts))
    row_trust = jnp.dot(onehot, trust_ratio, precision=lax.Precision.HIGHEST)
    scaled_update = row_trust[:, None] * update
    new_master = master_weights - step_size * scaled_update
    params = new_master.astype(jnp.bfloat16)
    stacked = params.reshape(1, 1, 1, own_rows, row_width)
    stacked = lax.all_gather(stacked, "gz", axis=2, tiled=True)
    stacked = lax.all_gather(stacked, "gy", axis=1, tiled=True)
    stacked = lax.all_gather(stacked, "gx", axis=0, tiled=True)
    gathered = stacked.reshape(count_across * count_down * count_along * own_rows, row_width)
    return (new_master, new_first, new_second, scaled_update, gathered)


def solution(mesh):
    placed = (
        P(("gx", "gy", "gz"), None, None),
        P(("gx", "gy", "gz"), None),
        P(("gx", "gy", "gz"), None),
        P(("gx", "gy", "gz"), None),
        P(("gx", "gy", "gz")),
    )
    return jax.shard_map(
        on_device,
        mesh=mesh,
        in_specs=placed,
        out_specs=(
            P(("gx", "gy", "gz"), None),
            P(("gx", "gy", "gz"), None),
            P(("gx", "gy", "gz"), None),
            P(("gx", "gy", "gz"), None),
            P(),
        ),
        check_vma=False,
    )
```

profile of v0, /device:TPU:0, one launch (start us, length us, event | category | flops | bytes accessed | tf_op | source)
XLA Modules:
  0.0 192.9 jit_solution(224679185084797779)
XLA Ops:
  7.2 0.0 copy-start.3
  7.2 0.0 copy-start
  7.2 0.0 copy-start.1
  7.2 0.0 copy-start.2
  7.2 0.0 reduce-scatter.2.cloned.1.call-start
  7.3 2.5 %bitcast_convert_fusion = f32[768,512]{1,0:T(8,128)} fusion(bf16[1,768,512]{2,1,0:T(8,128)(2,1)} %param.5), kind=kLoop, calls=%fused_computation.4 | loop fusion | flops 393216 | bytes 2359296 | tf_op jit(solution)/shard_map/convert_element_type | solution.py:23
  9.8 0.0 reduce-scatter.2.cloned.1.call-update
  9.8 0.0 copy-done.3
  9.8 0.1 convert_reduce_fusion
  9.9 104.0 %reduce-scatter.2.cloned.1.call-done = f32[24,512]{1,0:T(8,128)} async-done(((f32[768,512]{1,0:T(8,128)}), f32[24,512]{1,0:T(8,128)}) %reduce-scatter.2.cloned.1.call-update) | async-done | bytes 49168 | tf_op jit(solution)/shard_map/reduce_scatter | solution.py:27
  113.9 0.0 copy-done
  113.9 0.0 copy-done.1
  113.9 0.0 copy-done.2
  113.9 1.6 multiply_reduce_fusion
  115.5 0.1 fusion
  115.6 0.1 convolution_bitcast_fusion.2
  115.7 40.1 %all-reduce = (f32[4]{0:T(128)S(1)}, f32[4]{0:T(128)S(1)}) all-reduce(f32[4]{0:T(128)S(1)} %convolution_bitcast_fusion.2, f32[4]{0:T(128)S(1)} %fusion), channel_id=1, replica_groups=mesh['gx'=4,'gy'=4,'gz'=2] {'gx','gy','gz'}, use_global_device_ids=true, to_apply=%region_1.0 | all-reduce | flops 8 | bytes 64 | tf_op jit(solution)/shard_map/psum | solution.py:32
  155.8 0.1 convolution_bitcast_fusion
  155.9 0.7 fusion.8
  156.6 4.7 %all-gather = bf16[48,512]{1,0:T(8,128)(2,1)S(1)} all-gather(bf16[24,512]{1,0:T(8,128)(2,1)S(1)} %get-tuple-element.7), channel_id=2, replica_groups=mesh['gx'=4,'gy'=4,'gz'=2] {'gz'}, dimensions={0}, use_global_device_ids=true | all-gather | bytes 73728 | tf_op jit(solution)/shard_map/all_gather | solution.py:41
  161.4 5.9 %all_gather.10 = bf16[1,4,2,24,512]{4,3,2,0,1:T(8,128)(2,1)S(1)} all-gather(bf16[1,1,2,24,512]{4,3,2,0,1:T(8,128)(2,1)S(1)} %bitcast.25), channel_id=1, replica_groups=mesh['gx'=4,'gy'=4,'gz'=2] {'gy'}, dimensions={1}, use_global_device_ids=true | all-gather | bytes 245760 | tf_op jit(solution)/shard_map/all_gather | solution.py:42
  167.3 17.9 %all_gather.11 = bf16[4,4,2,24,512]{4,3,2,1,0:T(8,128)(2,1)S(1)} all-gather(bf16[1,4,2,24,512]{4,3,2,1,0:T(8,128)(2,1)S(1)} %bitcast.24), channel_id=1, replica_groups=mesh['gx'=4,'gy'=4,'gz'=2] {'gx'}, dimensions={0}, use_global_device_ids=true | all-gather | bytes 983040 | tf_op jit(solution)/shard_map/all_gather | solution.py:43
  185.2 0.9 copy.13
Async XLA Ops:
  7.2 2.6 %copy-start.3 = (s32[24]{0:T(128)S(1)}, s32[24]{0:T(128)}, u32[]{:S(2)}) copy-start(s32[24]{0:T(128)} %param.9) | copy-start | bytes 292
  7.2 106.7 %copy-start = (f32[24,512]{1,0:T(8,128)S(1)}, f32[24,512]{1,0:T(8,128)}, u32[]{:S(2)}) copy-start(f32[24,512]{1,0:T(8,128)} %param.6) | copy-start | bytes 147460
  7.2 106.7 %copy-start.1 = (f32[24,512]{1,0:T(8,128)S(1)}, f32[24,512]{1,0:T(8,128)}, u32[]{:S(2)}) copy-start(f32[24,512]{1,0:T(8,128)} %param.8) | copy-start | bytes 147460
  7.2 106.7 %copy-start.2 = (f32[24,512]{1,0:T(8,128)S(1)}, f32[24,512]{1,0:T(8,128)}, u32[]{:S(2)}) copy-start(f32[24,512]{1,0:T(8,128)} %param.7) | copy-start | bytes 147460
  7.2 106.7 %reduce-scatter.2.cloned.1.call-start = ((), (), s32[]{:S(2)}) async-start(), calls=%async_computation.1 | async-start | bytes 1622016 | tf_op jit(solution)/shard_map/reduce_scatter | solution.py:27
Sparse Core Ops, SparseCore 0:
  13.3 100.5 reduce-scatter.1
where the time goes:
time: 193 us
  waiting for transfers between devices  104 us (54%)
  blocking collectives  68.6 us (36%)
  between operations  14.1 us (7%)
  other arithmetic  4.92 us (3%)
    reduce_scatter x1, waiting for transfers between devices, on_device(): lax.psum_scatter(own_gradient, ('gx', 'gy', 'gz'), scatter_dimension=0, t...  104 us
    psum x1, blocking collectives, on_device(): lax.psum((weight_local, update_local, counts), ('gx', 'gy', 'gz'))  40.1 us
    all_gather x1, blocking collectives, on_device(): stacked = lax.all_gather(stacked, 'gx', axis=0, tiled=True)  17.9 us
    all_gather x1, blocking collectives, on_device(): stacked = lax.all_gather(stacked, 'gy', axis=1, tiled=True)  5.92 us
    all_gather x1, blocking collectives, on_device(): stacked = lax.all_gather(stacked, 'gz', axis=2, tiled=True)  4.72 us
  transfers between devices with their start and end apart: 1, of which 1 were waited for; matrix products, arithmetic and copies ran while one was open for 0% of the time, Pallas kernels for 0%

commit v1 on v0

--- a/solution.py
+++ b/solution.py
@@ -30,7 +30,7 @@
     update = new_first / (jnp.sqrt(new_second) + epsilon) + weight_decay * master_weights
     update_local = tensor_sums(update, onehot)
     weight_sq, update_sq, total_counts = lax.psum(
-        (weight_local, update_local, counts), ("gx", "gy", "gz")
+        lax.psum((weight_local, update_local, counts), ("gy", "gz")), "gx"
     )
     trust_ratio = jnp.sqrt(weight_sq / (update_sq + total_counts))
     row_trust = jnp.dot(onehot, trust_ratio, precision=lax.Precision.HIGHEST)

time: 193 us -> 176 us (0.912)
  blocking collectives: 68.6 us -> 51.9 us
    psum x1 -> x2, blocking collectives: 40.1 us -> 24.1 us  [the longest x1 13.4 us: on_device(): lax.psum((weight_local, update_local, counts), ('gy', 'gz'))]
where the time goes in v1:
time: 176 us
  waiting for transfers between devices  104 us (59%)
  blocking collectives  51.9 us (29%)
  between operations  14.1 us (8%)
  other arithmetic  4.92 us (3%)
    reduce_scatter x1, waiting for transfers between devices, on_device(): lax.psum_scatter(own_gradient, ('gx', 'gy', 'gz'), scatter_dimension=0, t...  104 us
    all_gather x1, blocking collectives, on_device(): stacked = lax.all_gather(stacked, 'gx', axis=0, tiled=True)  17.7 us
    psum x1, blocking collectives, on_device(): lax.psum((weight_local, update_local, counts), ('gy', 'gz'))  13.4 us
    psum x1, blocking collectives, on_device(): lax.psum(lax.psum((weight_local, update_local, counts), ('gy', 'gz')), 'gx')  10.7 us
    all_gather x1, blocking collectives, on_device(): stacked = lax.all_gather(stacked, 'gy', axis=1, tiled=True)  5.58 us
    all_gather x1, blocking collectives, on_device(): stacked = lax.all_gather(stacked, 'gz', axis=2, tiled=True)  4.48 us
  transfers between devices with their start and end apart: 1, of which 1 were waited for; matrix products, arithmetic and copies ran while one was open for 0% of the time, Pallas kernels for 0%

profile of v1, /device:TPU:0, one launch (start us, length us, event | category | flops | bytes accessed | tf_op | source)
XLA Modules:
  0.0 176.2 jit_solution(2148480315237815568)
XLA Ops:
  7.2 0.0 copy-start.3
  7.2 0.0 copy-start
  7.2 0.0 copy-start.1
  7.2 0.0 copy-start.2
  7.2 0.0 reduce-scatter.2.cloned.1.call-start
  7.3 2.5 %bitcast_convert_fusion = f32[768,512]{1,0:T(8,128)} fusion(bf16[1,768,512]{2,1,0:T(8,128)(2,1)} %param.5), kind=kLoop, calls=%fused_computation.4 | loop fusion | flops 393216 | bytes 2359296 | tf_op jit(solution)/shard_map/convert_element_type | solution.py:23
  9.8 0.0 reduce-scatter.2.cloned.1.call-update
  9.8 0.0 copy-done.3
  9.8 0.1 convert_reduce_fusion
  9.9 104.0 %reduce-scatter.2.cloned.1.call-done = f32[24,512]{1,0:T(8,128)} async-done(((f32[768,512]{1,0:T(8,128)}), f32[24,512]{1,0:T(8,128)}) %reduce-scatter.2.cloned.1.call-update) | async-done | bytes 49168 | tf_op jit(solution)/shard_map/reduce_scatter | solution.py:27
  113.9 0.0 copy-done
  113.9 0.0 copy-done.1
  113.9 0.0 copy-done.2
  113.9 1.6 multiply_reduce_fusion
  115.5 0.1 fusion
  115.6 0.1 convolution_bitcast_fusion.2
  115.7 13.4 %all-reduce = (f32[4]{0:T(128)S(1)}, f32[4]{0:T(128)S(1)}) all-reduce(f32[4]{0:T(128)S(1)} %convolution_bitcast_fusion.2, f32[4]{0:T(128)S(1)} %fusion), channel_id=1, replica_groups=mesh['gx'=4,'gy'=4,'gz'=2] {'gy','gz'}, use_global_device_ids=true, to_apply=%region_1.0 | all-reduce | flops 8 | bytes 64 | tf_op jit(solution)/shard_map/psum | solution.py:33
  129.1 10.7 %all-reduce.1 = (f32[4]{0:T(128)S(1)}, f32[4]{0:T(128)S(1)}) all-reduce(f32[4]{0:T(128)S(1)} %get-tuple-element.5, f32[4]{0:T(128)S(1)} %get-tuple-element.6), channel_id=1, replica_groups=mesh['gx'=4,'gy'=4,'gz'=2] {'gx'}, use_global_device_ids=true, to_apply=%region_2.0 | all-reduce | flops 8 | bytes 64 | tf_op jit(solution)/shard_map/psum | solution.py:32
  139.8 0.1 convolution_bitcast_fusion
  139.9 0.7 fusion.8
  140.7 4.5 %all-gather = bf16[48,512]{1,0:T(8,128)(2,1)S(1)} all-gather(bf16[24,512]{1,0:T(8,128)(2,1)S(1)} %get-tuple-element.9), channel_id=2, replica_groups=mesh['gx'=4,'gy'=4,'gz'=2] {'gz'}, dimensions={0}, use_global_device_ids=true | all-gather | bytes 73728 | tf_op jit(solution)/shard_map/all_gather | solution.py:41
  145.1 5.6 %all_gather.10 = bf16[1,4,2,24,512]{4,3,2,0,1:T(8,128)(2,1)S(1)} all-gather(bf16[1,1,2,24,512]{4,3,2,0,1:T(8,128)(2,1)S(1)} %bitcast.25), channel_id=1, replica_groups=mesh['gx'=4,'gy'=4,'gz'=2] {'gy'}, dimensions={1}, use_global_device_ids=true | all-gather | bytes 245760 | tf_op jit(solution)/shard_map/all_gather | solution.py:42
  150.7 17.7 %all_gather.11 = bf16[4,4,2,24,512]{4,3,2,1,0:T(8,128)(2,1)S(1)} all-gather(bf16[1,4,2,24,512]{4,3,2,1,0:T(8,128)(2,1)S(1)} %bitcast.24), channel_id=1, replica_groups=mesh['gx'=4,'gy'=4,'gz'=2] {'gx'}, dimensions={0}, use_global_device_ids=true | all-gather | bytes 983040 | tf_op jit(solution)/shard_map/all_gather | solution.py:43
  168.5 0.9 copy.13
Async XLA Ops:
  7.2 2.6 %copy-start.3 = (s32[24]{0:T(128)S(1)}, s32[24]{0:T(128)}, u32[]{:S(2)}) copy-start(s32[24]{0:T(128)} %param.9) | copy-start | bytes 292
  7.2 106.7 %copy-start = (f32[24,512]{1,0:T(8,128)S(1)}, f32[24,512]{1,0:T(8,128)}, u32[]{:S(2)}) copy-start(f32[24,512]{1,0:T(8,128)} %param.6) | copy-start | bytes 147460
  7.2 106.7 %copy-start.1 = (f32[24,512]{1,0:T(8,128)S(1)}, f32[24,512]{1,0:T(8,128)}, u32[]{:S(2)}) copy-start(f32[24,512]{1,0:T(8,128)} %param.8) | copy-start | bytes 147460
  7.2 106.7 %copy-start.2 = (f32[24,512]{1,0:T(8,128)S(1)}, f32[24,512]{1,0:T(8,128)}, u32[]{:S(2)}) copy-start(f32[24,512]{1,0:T(8,128)} %param.7) | copy-start | bytes 147460
  7.2 106.7 %reduce-scatter.2.cloned.1.call-start = ((), (), s32[]{:S(2)}) async-start(), calls=%async_computation.1 | async-start | bytes 1622016 | tf_op jit(solution)/shard_map/reduce_scatter | solution.py:27
Sparse Core Ops, SparseCore 0:
  13.3 100.5 reduce-scatter.1

commit v2 on v0

--- a/solution.py
+++ b/solution.py
@@ -40,7 +40,12 @@
     stacked = params.reshape(1, 1, 1, own_rows, row_width)
     stacked = lax.all_gather(stacked, "gz", axis=2, tiled=True)
     stacked = lax.all_gather(stacked, "gy", axis=1, tiled=True)
-    stacked = lax.all_gather(stacked, "gx", axis=0, tiled=True)
+    ring = [stacked]
+    for hop in range(3):
+        ring.append(lax.ppermute(ring[-1], "gx", [(dev, (dev + 1) % 4) for dev in range(4)]))
+    stacked = jnp.roll(
+        jnp.concatenate(ring[::-1], axis=0), (lax.axis_index("gx") + 1) * ring[0].shape[0], axis=0
+    )
     gathered = stacked.reshape(count_across * count_down * count_along * own_rows, row_width)
     return (new_master, new_first, new_second, scaled_update, gathered)
 

time: 193 us -> 200 us (1.036)
  waiting for transfers between devices: 104 us -> 128 us
  blocking collectives: 68.6 us -> 50.7 us
    ppermute x0 -> x3, waiting for transfers between devices: none -> 24.1 us  [on_device(): lax.ppermute(ring[-1], 'gx', [(dev, (dev + 1) % 4) for dev in range(4)])]
    all_gather x1 -> x0, blocking collectives: 17.9 us -> none  [on_device(): stacked = lax.all_gather(stacked, 'gx', axis=0, tiled=True)]
  transfers between devices with their start and end apart: 1 -> 4, of which waited for: 1 -> 4; matrix products, arithmetic and copies ran while one was open for 0% -> 0% of each run, Pallas kernels for 0% -> 0%
where the time goes in v2:
time: 200 us
  waiting for transfers between devices  128 us (64%)
  blocking collectives  50.7 us (25%)
  between operations  14.1 us (7%)
  other arithmetic  4.92 us (2%)
    reduce_scatter x1, waiting for transfers between devices, on_device(): lax.psum_scatter(own_gradient, ('gx', 'gy', 'gz'), scatter_dimension=0, t...  104 us
    psum x1, blocking collectives, on_device(): lax.psum((weight_local, update_local, counts), ('gx', 'gy', 'gz'))  40.1 us
    ppermute x3, waiting for transfers between devices, on_device(): lax.ppermute(ring[-1], 'gx', [(dev, (dev + 1) % 4) for dev in range(4)])  24.1 us
    all_gather x1, blocking collectives, on_device(): stacked = lax.all_gather(stacked, 'gy', axis=1, tiled=True)  5.92 us
    all_gather x1, blocking collectives, on_device(): stacked = lax.all_gather(stacked, 'gz', axis=2, tiled=True)  4.72 us
  transfers between devices with their start and end apart: 4, of which 4 were waited for; matrix products, arithmetic and copies ran while one was open for 0% of the time, Pallas kernels for 0%

profile of v2, /device:TPU:0, one launch (start us, length us, event | category | flops | bytes accessed | tf_op | source)
XLA Modules:
  0.0 199.8 jit_solution(5452996147087872939)
XLA Ops:
  7.2 0.0 copy-start.3
  7.2 0.0 copy-start
  7.2 0.0 copy-start.1
  7.2 0.0 copy-start.2
  7.2 0.0 reduce-scatter.2.cloned.1.call-start
  7.3 2.5 %bitcast_convert_fusion = f32[768,512]{1,0:T(8,128)} fusion(bf16[1,768,512]{2,1,0:T(8,128)(2,1)} %param.5), kind=kLoop, calls=%fused_computation.4 | loop fusion | flops 393216 | bytes 2359296 | tf_op jit(solution)/shard_map/convert_element_type | solution.py:23
  9.8 0.0 reduce-scatter.2.cloned.1.call-update
  9.8 0.0 copy-done.3
  9.8 0.1 convert_reduce_fusion
  9.9 104.0 %reduce-scatter.2.cloned.1.call-done = f32[24,512]{1,0:T(8,128)} async-done(((f32[768,512]{1,0:T(8,128)}), f32[24,512]{1,0:T(8,128)}) %reduce-scatter.2.cloned.1.call-update) | async-done | bytes 49168 | tf_op jit(solution)/shard_map/reduce_scatter | solution.py:27
  113.9 0.0 copy-done
  113.9 0.0 copy-done.1
  113.9 0.0 copy-done.2
  113.9 1.6 multiply_reduce_fusion
  115.5 0.1 fusion
  115.6 0.1 convolution_bitcast_fusion.2
  115.7 40.1 %all-reduce = (f32[4]{0:T(128)S(1)}, f32[4]{0:T(128)S(1)}) all-reduce(f32[4]{0:T(128)S(1)} %convolution_bitcast_fusion.2, f32[4]{0:T(128)S(1)} %fusion), channel_id=1, replica_groups=mesh['gx'=4,'gy'=4,'gz'=2] {'gx','gy','gz'}, use_global_device_ids=true, to_apply=%region_1.0 | all-reduce | flops 8 | bytes 64 | tf_op jit(solution)/shard_map/psum | solution.py:32
  155.8 0.1 convolution_bitcast_fusion
  155.9 0.7 fusion.8
  156.6 4.7 %all-gather = bf16[48,512]{1,0:T(8,128)(2,1)S(1)} all-gather(bf16[24,512]{1,0:T(8,128)(2,1)S(1)} %get-tuple-element.7), channel_id=2, replica_groups=mesh['gx'=4,'gy'=4,'gz'=2] {'gz'}, dimensions={0}, use_global_device_ids=true | all-gather | bytes 73728 | tf_op jit(solution)/shard_map/all_gather | solution.py:41
  161.4 5.9 %all_gather.7 = bf16[1,4,2,24,512]{4,3,2,0,1:T(8,128)(2,1)S(1)} all-gather(bf16[1,1,2,24,512]{4,3,2,0,1:T(8,128)(2,1)S(1)} %bitcast.29), channel_id=1, replica_groups=mesh['gx'=4,'gy'=4,'gz'=2] {'gy'}, dimensions={1}, use_global_device_ids=true | all-gather | bytes 245760 | tf_op jit(solution)/shard_map/all_gather | solution.py:42
  167.3 0.4 collective-permute-start
  167.7 8.5 %collective-permute-done = bf16[1,4,2,24,512]{4,3,2,1,0:T(8,128)(2,1)S(1)} collective-permute-done((bf16[1,4,2,24,512]{4,3,2,1,0:T(8,128)(2,1)S(1)}, bf16[1,4,2,24,512]{4,3,2,1,0:T(8,128)(2,1)S(1)}, u32[]{:S(2)}, u32[]{:S(2)}) %collective-permute-start) | collective-permute-done | bytes 196640 | tf_op jit(solution)/shard_map/ppermute | solution.py:45
  176.2 0.0 collective-permute-start.1
  176.2 8.1 %collective-permute-done.1 = bf16[1,4,2,24,512]{4,3,2,1,0:T(8,128)(2,1)S(1)} collective-permute-done((bf16[1,4,2,24,512]{4,3,2,1,0:T(8,128)(2,1)S(1)}, bf16[1,4,2,24,512]{4,3,2,1,0:T(8,128)(2,1)S(1)}, u32[]{:S(2)}, u32[]{:S(2)}) %collective-permute-start.1) | collective-permute-done | bytes 196640 | tf_op jit(solution)/shard_map/ppermute | solution.py:45
  184.3 0.0 collective-permute-start.2
  184.3 7.5 %collective-permute-done.2 = bf16[1,4,2,24,512]{4,3,2,1,0:T(8,128)(2,1)S(1)} collective-permute-done((bf16[1,4,2,24,512]{4,3,2,1,0:T(8,128)(2,1)S(1)}, bf16[1,4,2,24,512]{4,3,2,1,0:T(8,128)(2,1)S(1)}, u32[]{:S(2)}, u32[]{:S(2)}) %collective-permute-start.2) | collective-permute-done | bytes 196640 | tf_op jit(solution)/shard_map/ppermute | solution.py:45
  192.0 1.0 constant_dynamic-slice_fusion
  (8 shorter events, 0.1 us)
Async XLA Ops:
  7.2 2.6 %copy-start.3 = (s32[24]{0:T(128)S(1)}, s32[24]{0:T(128)}, u32[]{:S(2)}) copy-start(s32[24]{0:T(128)} %param.9) | copy-start | bytes 292
  7.2 106.7 %copy-start = (f32[24,512]{1,0:T(8,128)S(1)}, f32[24,512]{1,0:T(8,128)}, u32[]{:S(2)}) copy-start(f32[24,512]{1,0:T(8,128)} %param.6) | copy-start | bytes 147460
  7.2 106.7 %copy-start.1 = (f32[24,512]{1,0:T(8,128)S(1)}, f32[24,512]{1,0:T(8,128)}, u32[]{:S(2)}) copy-start(f32[24,512]{1,0:T(8,128)} %param.8) | copy-start | bytes 147460
  7.2 106.7 %copy-start.2 = (f32[24,512]{1,0:T(8,128)S(1)}, f32[24,512]{1,0:T(8,128)}, u32[]{:S(2)}) copy-start(f32[24,512]{1,0:T(8,128)} %param.7) | copy-start | bytes 147460
  7.2 106.7 %reduce-scatter.2.cloned.1.call-start = ((), (), s32[]{:S(2)}) async-start(), calls=%async_computation.1 | async-start | bytes 1622016 | tf_op jit(solution)/shard_map/reduce_scatter | solution.py:27
  167.3 8.9 %collective-permute-start = (bf16[1,4,2,24,512]{4,3,2,1,0:T(8,128)(2,1)S(1)}, bf16[1,4,2,24,512]{4,3,2,1,0:T(8,128)(2,1)S(1)}, u32[]{:S(2)}, u32[]{:S(2)}) collective-permute-start(bf16[1,4,2,24,512]{4,3,2,1,0:T(8,128)(2,1)S(1)} %bitcast.27), channel_id=1, source_target_pairs={{0,8},{8,16},{16,24},{24,0},{1,9},{9,17},{17,25},{25,1},{2,10},{10... | collective-permute-start | bytes 589832 | tf_op jit(solution)/shard_map/ppermute | solution.py:45
  176.2 8.1 %collective-permute-start.1 = (bf16[1,4,2,24,512]{4,3,2,1,0:T(8,128)(2,1)S(1)}, bf16[1,4,2,24,512]{4,3,2,1,0:T(8,128)(2,1)S(1)}, u32[]{:S(2)}, u32[]{:S(2)}) collective-permute-start(bf16[1,4,2,24,512]{4,3,2,1,0:T(8,128)(2,1)S(1)} %collective-permute-done), channel_id=1, source_target_pairs={{0,8},{8,16},{16,24},{24,0},{1,9},{9,17},{17,25},{25,1},{2,10},{10... | collective-permute-start | bytes 589832 | tf_op jit(solution)/shard_map/ppermute | solution.py:45
  184.3 7.5 %collective-permute-start.2 = (bf16[1,4,2,24,512]{4,3,2,1,0:T(8,128)(2,1)S(1)}, bf16[1,4,2,24,512]{4,3,2,1,0:T(8,128)(2,1)S(1)}, u32[]{:S(2)}, u32[]{:S(2)}) collective-permute-start(bf16[1,4,2,24,512]{4,3,2,1,0:T(8,128)(2,1)S(1)} %collective-permute-done.1), channel_id=1, source_target_pairs={{0,8},{8,16},{16,24},{24,0},{1,9},{9,17},{17,25},{25,1},{2,10},{10... | collective-permute-start | bytes 589832 | tf_op jit(solution)/shard_map/ppermute | solution.py:45
Sparse Core Ops, SparseCore 0:
  13.3 100.5 reduce-scatter.1
